TPU v7x, 32 devices: a whole 2x2x4 slice. The times are simulated.
32 devices in a mesh: seq: 16 (over z, y, core), head: 2 (over x).
Axes of the slice: x: 2, y: 2, z: 4, core: 2. Of those that a mesh axis runs over, the one named last changes fastest.
Arguments:
- image_in: bfloat16 [16384, 768], P(('seq', 'head')), may hold values from -6 to 6
- ln_gain: float32 [768], replicated, may hold values from 0.5 to 1.5
- w_in: bfloat16 [768, 5376], replicated, may hold values from -0.21875 to 0.21875
- q_gain: float32 [64], replicated, may hold values from 0.8 to 1.6
- k_gain: float32 [64], replicated, may hold values from 0.8 to 1.6
- w_attn_out: bfloat16 [768, 768], replicated, may hold values from -0.75 to 0.75
- w_mlp_out: bfloat16 [3072, 768], replicated, may hold values from -0.109375 to 0.109375
- cotangent: bfloat16 [16384, 768], P(('seq', 'head')), may hold values from -6 to 6
- image_ids: int32 [16, 1024], P('seq'), may hold values from 0 to 15, never falling along the last dimension, each value on 1 to 768 neighbouring positions
Outputs:
- block_out: bfloat16 [16384, 768], P(('seq', 'head'))
- grad_image: float32 [16384, 768], P(('seq', 'head'))
- grad_ln_gain: float32 [768], replicated
- grad_w_in: float32 [768, 5376], replicated
- grad_q_gain: float32 [64], replicated
- grad_k_gain: float32 [64], replicated
- grad_w_attn_out: float32 [768, 768], replicated
- grad_w_mlp_out: float32 [3072, 768], replicated
Inputs may be any that keep to these rules, and one draw needn't show every extreme that they name: `image_ids`: along each row the ids never fall; the tokens of one image form a run of equal ids within one row; an image has 1 to 768 tokens, and in each row one image has exactly 768.
All inputs are finite; a program needn't handle non-finite values.
Results may differ from a plain program's by a relative error of at most 0.012.
Values may be sent and summed in bfloat16 or wider, within the bound.
No kernel may reach another device: no remote copies, remote signals or barrier semaphores. Data moves between devices by JAX's collectives and lax.ppermute only.
A program may use at most 192 MiB of HBM per device.

v0:
```python
import jax
import jax.numpy as jnp
from jax import lax
from jax.sharding import PartitionSpec as P

norm_epsilon = 1e-06


def norm_rows(values, gain):
    center = values - jnp.mean(values, axis=-1, keepdims=True)
    spread = jnp.mean(center * center, axis=-1, keepdims=True)
    return center * lax.rsqrt(spread + norm_epsilon) * gain


def qk_norms(raw_query, raw_key, gain_query, gain_key):
    return (norm_rows(raw_query, gain_query), norm_rows(raw_key, gain_key))


def across_rows(left, right):
    return lax.dot_general(
        left, right, (((0,), (0,)), ((), ())), preferred_element_type=jnp.float32
    )


def against_cols(left, right):
    return lax.dot_general(
        left, right, (((1,), (1,)), ((), ())), preferred_element_type=jnp.float32
    )


def head_side(heads, q_gain, k_gain):
    (query_f32, key_f32), qk_pull = jax.vjp(
        qk_norms, heads[:, 0].astype(jnp.float32), heads[:, 1].astype(jnp.float32), q_gain, k_gain
    )
    return (query_f32.astype(jnp.bfloat16), key_f32.astype(jnp.bfloat16), heads[:, 2], qk_pull)


def masked_scores(query_rows, id_rows, keys_all, row_ids):
    raw_scores = (
        jnp.einsum("rhe,ghe->hrg", query_rows, keys_all, preferred_element_type=jnp.float32) * 0.125
    )
    same_image = id_rows[:, None] == row_ids[None, :]
    return jnp.where(same_image[None], raw_scores, -1e30)


def per_device(
    image_in, ln_gain, w_in, q_gain, k_gain, w_attn_out, w_mlp_out, cotangent, image_ids
):
    tokens_here = image_in.shape[0]
    span = w_attn_out.shape[0]
    head_size = q_gain.shape[0]
    pairs = lax.axis_size("head")
    local_heads = span // head_size // pairs
    part_cols = span // pairs
    image_f32 = image_in.astype(jnp.float32)
    normed_f32, norm_pull = jax.vjp(norm_rows, image_f32, ln_gain)
    normed_low = normed_f32.astype(jnp.bfloat16)
    proj = jnp.dot(normed_low, w_in, preferred_element_type=jnp.float32)
    qkv_low = proj[:, : 3 * span].astype(jnp.bfloat16)
    upper = proj[:, 3 * span :]
    act_f32, gelu_pull = jax.vjp(lambda inner: jax.nn.gelu(inner, approximate=False), upper)
    act_low = act_f32.astype(jnp.bfloat16)
    sent = qkv_low.reshape(tokens_here, 3, pairs, part_cols)
    heads = lax.all_to_all(sent, "head", split_axis=2, concat_axis=0, tiled=True)
    group_len = heads.shape[0]
    heads = heads.reshape(group_len, 3, local_heads, head_size)
    row_ids = image_ids[0]
    block_rows = min(512, group_len)
    block_count = group_len // block_rows
    id_blocks = row_ids.reshape(block_count, block_rows)
    queries, keys_all, values_all, qk_pull = head_side(heads, q_gain, k_gain)

    def forward_block(block_pair):
        query_rows, id_rows = block_pair
        masked = masked_scores(query_rows, id_rows, keys_all, row_ids)
        top_score = jnp.max(masked, axis=-1, keepdims=True)
        expd = jnp.exp(masked - top_score)
        totals = jnp.sum(expd, axis=-1, keepdims=True)
        weights = (expd / totals).astype(jnp.bfloat16)
        outputs = jnp.einsum(
            "hrg,ghe->rhe", weights, values_all, preferred_element_type=jnp.float32
        )
        return (outputs, (top_score + jnp.log(totals))[..., 0])

    query_blocks = queries.reshape(block_count, block_rows, local_heads, head_size)
    out_blocks, log_total = lax.map(forward_block, (query_blocks, id_blocks))
    attended_heads = out_blocks.reshape(group_len, 1, part_cols).astype(jnp.bfloat16)
    back_tokens = lax.all_to_all(attended_heads, "head", split_axis=0, concat_axis=1, tiled=True)
    attended = back_tokens.reshape(tokens_here, span)
    branch = jnp.dot(attended, w_attn_out, preferred_element_type=jnp.float32)
    branch = branch + jnp.dot(act_low, w_mlp_out, preferred_element_type=jnp.float32)
    block_out = (image_f32 + branch).astype(jnp.bfloat16)
    grad_attn_w = across_rows(attended, cotangent)
    grad_mlp_w = across_rows(act_low, cotangent)
    d_attended = against_cols(cotangent, w_attn_out).astype(jnp.bfloat16)
    d_act = against_cols(cotangent, w_mlp_out)
    d_upper = gelu_pull(d_act)[0].astype(jnp.bfloat16)
    d_heads = lax.all_to_all(
        d_attended.reshape(tokens_here, pairs, part_cols),
        "head",
        split_axis=1,
        concat_axis=0,
        tiled=True,
    )
    query_use, keys_use, values_use, pull_use = (queries, keys_all, values_all, qk_pull)
    d_heads = d_heads.reshape(group_len, local_heads, head_size)

    def backward_block(carry, block_items):
        key_grad, value_grad = carry
        query_rows, id_rows, total_rows, grad_rows = block_items
        masked = masked_scores(query_rows, id_rows, keys_use, row_ids)
        probs = jnp.exp(masked - total_rows[..., None])
        weights = probs.astype(jnp.bfloat16)
        value_grad = value_grad + jnp.einsum(
            "hrg,rhe->ghe", weights, grad_rows, preferred_element_type=jnp.float32
        )
        d_probs = jnp.einsum(
            "rhe,ghe->hrg", grad_rows, values_use, preferred_element_type=jnp.float32
        )
        centre = jnp.sum(probs * d_probs, axis=-1, keepdims=True)
        d_scores = (probs * (d_probs - centre)).astype(jnp.bfloat16)
        query_grad = (
            jnp.einsum("hrg,ghe->rhe", d_scores, keys_use, preferred_element_type=jnp.float32)
            * 0.125
        )
        key_grad = (
            key_grad
            + jnp.einsum("hrg,rhe->ghe", d_scores, query_rows, preferred_element_type=jnp.float32)
            * 0.125
        )
        return ((key_grad, value_grad), query_grad)

    zeros_heads = jnp.zeros((group_len, local_heads, head_size), jnp.float32)
    block_items = (
        query_use.reshape(block_count, block_rows, local_heads, head_size),
        id_blocks,
        log_total,
        d_heads.reshape(block_count, block_rows, local_heads, head_size),
    )
    (key_grad, value_grad), query_grads = lax.scan(
        backward_block, (zeros_heads, zeros_heads), block_items
    )
    query_grad = query_grads.reshape(group_len, local_heads, head_size)
    d_query, d_key, grad_qg, grad_kg = pull_use((query_grad, key_grad))
    d_qkv_heads = jnp.stack([d_query, d_key, value_grad], axis=1).astype(jnp.bfloat16)
    d_qkv_heads = d_qkv_heads.reshape(group_len, 3, 1, part_cols)
    d_qkv = lax.all_to_all(d_qkv_heads, "head", split_axis=0, concat_axis=2, tiled=True)
    d_proj = jnp.concatenate([d_qkv.reshape(tokens_here, 3 * span), d_upper], axis=1)
    grad_win = across_rows(normed_low, d_proj)
    d_normed = against_cols(d_proj, w_in)
    d_input, grad_lng = norm_pull(d_normed)
    grad_image = cotangent.astype(jnp.float32) + d_input
    grad_win, grad_attn_w, grad_mlp_w, grad_lng, grad_qg, grad_kg = lax.psum(
        (grad_win, grad_attn_w, grad_mlp_w, grad_lng, grad_qg, grad_kg), ("seq", "head")
    )
    return (block_out, grad_image, grad_lng, grad_win, grad_qg, grad_kg, grad_attn_w, grad_mlp_w)


def solution(mesh):
    in_specs = (
        P(("seq", "head"), None),
        P(),
        P(),
        P(),
        P(),
        P(),
        P(),
        P(("seq", "head"), None),
        P("seq", None),
    )
    out_specs = (P(("seq", "head"), None), P(("seq", "head"), None), P(), P(), P(), P(), P(), P())
    return jax.shard_map(
        per_device, mesh=mesh, in_specs=in_specs, out_specs=out_specs, check_vma=False
    )
```

profile of v0, /device:TPU:0, one launch (start us, length us, event | category | flops | bytes accessed | tf_op | source)
XLA Modules:
  0.0 774.1 jit_solution(2545150310376141355)
XLA Ops:
  16.3 7.0 fusion.74
  40.7 19.5 %add_convert_fusion = (bf16[512,3072]{1,0:T(8,128)(2,1)}, f32[512,3072]{1,0:T(8,128)}) fusion(f32[512,5376]{1,0:T(8,128)} %copy-done.10, bf16[512,768]{1,0:T(8,128)(2,1)S(1)} %copy-done.15, bf16[3072,768]{1,0:T(8,128)(2,1)} %param.19), kind=kOutput, calls=%fused_computation.48 | convolution fusion | flops 2529165312 | bytes 21233664 | tf_op jit(solution)/shard_map/dot_general | solution.py:26
  63.6 6.4 all-to-all-done
  70.0 6.8 copy.80
  76.8 6.6 reshape.324
  99.0 27.2 %while.27 = (s32[]{:T(128)}, bf16[2,512,6,64]{1,3,2,0:T(8,128)(2,1)}, f32[2,6,512]{2,1,0:T(8,128)}, s32[2,512]{1,0:T(2,128)S(1)}, s32[1,1024]{1,0:T(1,128)S(1)},...) while((s32[]{:T(128)}, ...), condition=%wide.region_9.10_spmd, body=%wide.region_6.9_spmd.sunk | while | flops 843576320 | bytes 52361472 | solution.py:86
  126.2 86.7 %while.28 = (s32[]{:T(128)}, f32[1024,6,64]{0,2,1:T(8,128)S(1)}, f32[1024,6,64]{0,2,1:T(8,128)}, f32[2,512,6,64]{1,0,3,2:T(2,128)}, bf16[2,512,6,64]{1,3,2,0:T(8...) while((s32[]{:T(128)}, f32[1024,6,64]{0,2,1:T(8,128)S(1)}, ...), condition=%wide.region_12.13_spmd.clone, body=%wide.region_10.12_spmd.clone.sunk | while | flops 2063135744 | bytes 120166672 | solution.py:140
  134.9 7.2 multiply_reduce_fusion.5
  142.1 6.9 multiply_convert_fusion.4
  154.1 15.0 %dynamic_update_slice.19 = f32[2,512,6,64]{1,0,3,2:T(2,128)} dynamic-update-slice(f32[2,512,6,64]{1,0,3,2:T(2,128)} %get-tuple-element.481, f32[1,512,6,64]{1,0,3,2:T(1,128)} %copy.119, s32[]{:T(128)S(6)} %copy.136, s32[]{:T(128)} %constant.62.clone.1..sunk, s32[]{:T(128)} %constant.62.clone.1..sunk, s32[]{:T(128)} %constant.62.clone.1..sunk) | dynamic-update-slice | bytes 1572868 | tf_op jit(solution)/shard_map/while/body/jit(dynamic_update_index_in_dim)/dynamic_update_slice | solution.py:86
  173.1 5.8 bitcast_add_fusion.5
  178.9 7.2 multiply_reduce_fusion.5
  186.1 6.9 multiply_convert_fusion.4
  198.0 15.0 %dynamic_update_slice.19 = f32[2,512,6,64]{1,0,3,2:T(2,128)} dynamic-update-slice(f32[2,512,6,64]{1,0,3,2:T(2,128)} %get-tuple-element.481, f32[1,512,6,64]{1,0,3,2:T(1,128)} %copy.119, s32[]{:T(128)S(6)} %copy.136, s32[]{:T(128)} %constant.62.clone.1..sunk, s32[]{:T(128)} %constant.62.clone.1..sunk, s32[]{:T(128)} %constant.62.clone.1..sunk) | dynamic-update-slice | bytes 1572868 | tf_op jit(solution)/shard_map/while/body/jit(dynamic_update_index_in_dim)/dynamic_update_slice | solution.py:86
  241.8 5.5 multiply_reduce_fusion.1
  257.9 6.2 multiply_convert_fusion.1
  276.3 17.1 %all-to-all-done.3 = bf16[1024,3,1,384]{3,1,2,0:T(4,128)(2,1)} async-done(((bf16[1024,3,1,384]{3,1,2,0:T(4,128)(2,1)}), bf16[1024,3,1,384]{3,1,2,0:T(4,128)(2,1)}, u32[]{:S(2)}, u32[]{:S(2)}) %all-to-all-start.3) | async-done | bytes 2359328 | tf_op jit(solution)/shard_map/all_to_all | solution.py:147
  299.5 6.3 reshape.329
  305.8 11.4 %fusion.40 = f32[768,5376]{1,0:T(8,128)} fusion(bf16[512,3072]{1,0:T(8,128)(2,1)} %get-tuple-element.301, bf16[512,2304]{1,0:T(8,128)(2,1)} %reshape.329, bf16[512,768]{1,0:T(8,128)(2,1)S(1)} %copy-done.6, f32[768]{0:T(1024)S(1)} %copy-done.35, f32[512]{0:T(512)S(1)} %copy-done.47, f32[512]{0:T(512)S(1)} %copy-done.43), kind=kOutput, calls=%fused_computation.66 | convolution fusion | flops 4240834560 | bytes 22813696 | tf_op jit(solution)/shard_map/dot_general | solution.py:20
  317.3 6.0 fusion.78
  325.3 7.9 %fusion.62 = (f32[512]{0:T(512)S(1)}, f32[512,768]{1,0:T(8,128)S(1)}) fusion(bf16[512,768]{1,0:T(8,128)(2,1)S(1)} %copy-done.6, f32[768]{0:T(1024)S(1)} %copy-done.35, f32[512]{0:T(512)S(1)} %copy-done.43, bf16[768,5376]{1,0:T(8,128)(2,1)} %param.15, bf16[512,3072]{1,0:T(8,128)(2,1)S(1)} %copy-done.12, bf16[512,2304]{1,0:T(8,128)(2,1)S(1)} %copy-done.8), kind=kOutput, calls=%fused_computation.98 | convolution fusion | flops 4240834048 | bytes 16129024 | tf_op jit(solution)/shard_map/dot_general | solution.py:26
  334.6 41.6 %all-reduce = (f32[768]{0:T(1024)}, f32[64]{0:T(128)}, f32[64]{0:T(128)}) all-reduce(f32[768]{0:T(1024)} %get-tuple-element.250, f32[64]{0:T(128)} %get-tuple-element.248, f32[64]{0:T(128)} %get-tuple-element.246), channel_id=1, replica_groups=mesh['seq'=16,'head'=2] {'seq','head'}, use_global_device_ids=true, to_apply=%region_20.21 | all-reduce | flops 896 | bytes 7168 | tf_op jit(solution)/shard_map/psum | solution.py:153
  379.8 367.5 %all-reduce.4.cloned.1.call-done = (f32[768,5376]{1,0:T(8,128)}, f32[768,768]{1,0:T(8,128)}, f32[3072,768]{1,0:T(8,128)}) async-done(((f32[768,5376]{1,0:T(8,128)}, f32[768,768]{1,0:T(8,128)}, f32[3072,768]{1,0:T(8,128)}), (f32[768,5376]{1,0:T(8,128)}, f32[768,768]{1,0:T(8,128)}, f32[3072,768]{1,0:T(8,128)})) %all-reduce.4.cloned.1.call-update) | async-done | bytes 28311568 | tf_op jit(solution)/shard_map/psum | solution.py:153
  747.3 13.8 %copy.147 = f32[768,5376]{1,0:T(8,128)} copy(f32[768,5376]{1,0:T(8,128)} %get-tuple-element.507) | data formatting | bytes 33030144
  (226 shorter events, 165.0 us)
Async XLA Ops:
  7.2 8.5 %copy-start.5 = (bf16[512,768]{1,0:T(8,128)(2,1)S(1)}, bf16[512,768]{1,0:T(8,128)(2,1)}, u32[]{:S(2)}) copy-start(bf16[512,768]{1,0:T(8,128)(2,1)} %param.13) | copy-start | bytes 2359300
  11.4 24.1 %all-to-all-start.2 = ((bf16[512,2,384]{2,0,1:T(8,128)(2,1)}), bf16[512,2,384]{2,0,1:T(8,128)(2,1)}, u32[]{:S(2)}, u32[]{:S(2)}) async-start(bf16[512,2,384]{2,0,1:T(8,128)(2,1)} %bitcast.144), calls=%async_computation.2 | async-start | bytes 1572864 | tf_op jit(solution)/shard_map/all_to_all | solution.py:98
  15.9 7.4 copy-start.42
  35.5 34.6 %all-to-all-start = ((bf16[512,3,2,384]{3,0,1,2:T(8,128)(2,1)}), bf16[512,3,2,384]{3,0,1,2:T(8,128)(2,1)}, u32[]{:S(2)}, u32[]{:S(2)}) async-start(bf16[512,3,2,384]{3,0,1,2:T(8,128)(2,1)} %copy.79), calls=%async_computation | async-start | bytes 4718592 | tf_op jit(solution)/shard_map/all_to_all | solution.py:64
  40.7 20.0 %copy-start.28 = (s32[1,1024]{1,0:T(1,128)S(1)}, s32[1,1024]{1,0:T(1,128)}, u32[]{:S(2)}) copy-start(s32[1,1024]{1,0:T(1,128)} %param.21) | copy-start | bytes 12292
  88.1 8.5 %copy-start.18 = (f32[1024,6]{0,1:T(8,128)}, f32[1024,6]{0,1:T(8,128)S(1)}, u32[]{:S(2)}) copy-start(f32[1024,6]{0,1:T(8,128)S(1)} %broadcast_multiply_fusion) | copy-start | bytes 73732
  88.1 8.4 %copy-start.21 = (f32[1024,6]{0,1:T(8,128)}, f32[1024,6]{0,1:T(8,128)S(1)}, u32[]{:S(2)}) copy-start(f32[1024,6]{0,1:T(8,128)S(1)} %broadcast_multiply_fusion.1) | copy-start | bytes 73732
  88.2 8.4 %copy-start.36 = (f32[2,512,6]{1,0,2:T(2,128)}, f32[2,512,6]{1,0,2:T(2,128)S(1)}, u32[]{:S(2)}) copy-start(f32[2,512,6]{1,0,2:T(2,128)S(1)} %div.74) | copy-start | bytes 73732
  229.4 8.8 %copy-start.53 = (f32[64]{0:T(128)S(1)}, f32[64]{0:T(128)}, u32[]{:S(2)}) copy-start(f32[64]{0:T(128)} %param.16) | copy-start | bytes 772
  233.7 8.0 %copy-start.41 = (f32[2,512,6]{1,0,2:T(2,128)S(1)}, f32[2,512,6]{1,0,2:T(2,128)}, u32[]{:S(2)}) copy-start(f32[2,512,6]{1,0,2:T(2,128)} %copy-done.40) | copy-start | bytes 73732
  233.7 8.1 %copy-start.37 = (f32[2,512,6]{1,0,2:T(2,128)S(1)}, f32[2,512,6]{1,0,2:T(2,128)}, u32[]{:S(2)}) copy-start(f32[2,512,6]{1,0,2:T(2,128)} %copy-done.36) | copy-start | bytes 73732
  233.7 8.1 %copy-start.39 = (f32[2,512,6]{1,0,2:T(2,128)S(1)}, f32[2,512,6]{1,0,2:T(2,128)}, u32[]{:S(2)}) copy-start(f32[2,512,6]{1,0,2:T(2,128)} %copy-done.38) | copy-start | bytes 73732
  233.7 18.6 %all-to-all-start.1 = ((bf16[2,2,98304]{2,1,0:T(2,128)(2,1)}), bf16[2,2,98304]{2,1,0:T(2,128)(2,1)}, u32[]{:S(2)}, u32[]{:S(2)}) async-start(bf16[2,2,98304]{2,1,0:T(2,128)(2,1)} %reshape.340), calls=%async_computation.1 | async-start | bytes 1572864 | tf_op jit(solution)/shard_map/all_to_all | solution.py:88
  238.2 9.1 %copy-start.33 = (f32[1024,6]{0,1:T(8,128)S(1)}, f32[1024,6]{0,1:T(8,128)}, u32[]{:S(2)}) copy-start(f32[1024,6]{0,1:T(8,128)} %copy-done.32) | copy-start | bytes 73732
  238.2 9.2 %copy-start.20 = (f32[1024,6]{0,1:T(8,128)S(1)}, f32[1024,6]{0,1:T(8,128)}, u32[]{:S(2)}) copy-start(f32[1024,6]{0,1:T(8,128)} %copy-done.18) | copy-start | bytes 73732
  238.2 9.2 %copy-start.27 = (f32[1024,6]{0,1:T(8,128)S(1)}, f32[1024,6]{0,1:T(8,128)}, u32[]{:S(2)}) copy-start(f32[1024,6]{0,1:T(8,128)} %fusion.68) | copy-start | bytes 73732
  238.2 9.2 %copy-start.29 = (f32[1024,6]{0,1:T(8,128)S(1)}, f32[1024,6]{0,1:T(8,128)}, u32[]{:S(2)}) copy-start(f32[1024,6]{0,1:T(8,128)} %multiply_multiply_fusion.5) | copy-start | bytes 73732
  252.4 41.1 %all-to-all-start.3 = ((bf16[1024,3,1,384]{3,1,2,0:T(4,128)(2,1)}), bf16[1024,3,1,384]{3,1,2,0:T(4,128)(2,1)}, u32[]{:S(2)}, u32[]{:S(2)}) async-start(bf16[1024,3,1,384]{3,1,2,0:T(4,128)(2,1)} %copy.91), calls=%async_computation.3 | async-start | bytes 6291456 | tf_op jit(solution)/shard_map/all_to_all | solution.py:147
  257.6 489.7 %all-reduce.4.cloned.1.call-start = ((), (), s32[]{:S(2)}) async-start(), calls=%async_computation.4 | async-start | bytes 56623104 | tf_op jit(solution)/shard_map/psum | solution.py:153
  257.9 7.9 %copy-start.16 = (bf16[512,768]{1,0:T(8,128)(2,1)S(1)}, bf16[512,768]{1,0:T(8,128)(2,1)}, u32[]{:S(2)}) copy-start(bf16[512,768]{1,0:T(8,128)(2,1)} %param.20) | copy-start | bytes 2359300
  317.2 7.8 %copy-start.12 = (bf16[512,3072]{1,0:T(8,128)(2,1)S(1)}, bf16[512,3072]{1,0:T(8,128)(2,1)}, u32[]{:S(2)}) copy-start(bf16[512,3072]{1,0:T(8,128)(2,1)} %get-tuple-element.301) | copy-start | bytes 9437188
  325.3 7.9 %copy-start.49 = (f32[512]{0:T(512)S(1)}, f32[512]{0:T(512)}, u32[]{:S(2)}) copy-start(f32[512]{0:T(512)} %copy-done.48) | copy-start | bytes 6148
  747.3 13.8 %copy-start.17 = (f32[768,768]{1,0:T(8,128)S(1)}, f32[768,768]{1,0:T(8,128)}, u32[]{:S(2)}) copy-start(f32[768,768]{1,0:T(8,128)} %get-tuple-element.510) | copy-start | bytes 7077892
  747.3 15.9 %copy-start.9 = (f32[3072,768]{1,0:T(8,128)S(1)}, f32[3072,768]{1,0:T(8,128)}, u32[]{:S(2)}) copy-start(f32[3072,768]{1,0:T(8,128)} %get-tuple-element.511) | copy-start | bytes 28311556
  (43 other events, 187.1 us)
Sparse Core Ops, SparseCore 0:
  317.4 429.9 all-reduce.3
where the time goes:
time: 782 us; the launch traced here: 774 us
  waiting for transfers between devices  391 us (50%)
  local copies, waits for them, and re-layouts  127 us (16%)
  matrix products  117 us (15%)
  other arithmetic  62.5 us (8%)
  blocking collectives  41.6 us (5%)
  starting transfers between devices  19.4 us (2%)
  between operations  15 us (2%)
    psum x1, waiting for transfers between devices, per_device(): lax.psum((grad_win, grad_attn_w, grad_mlp_w, grad_lng, grad_qg, grad_kg),...  368 us
    psum x1, blocking collectives, per_device(): lax.psum((grad_win, grad_attn_w, grad_mlp_w, grad_lng, grad_qg, grad_kg),...  41.6 us
    dynamic_update_slice x4, local copies, waits for them, and re-layouts, per_device(): out_blocks, log_total = lax.map(forward_block, (query_blocks, id_blocks))  33.3 us
    unnamed x101, local copies, waits for them, and re-layouts  32.1 us
    dot_general x3, matrix products, against_cols(): lax.dot_general(left, right, (((1,), (1,)), ((), ())), preferred_element_...  29.3 us
    dot_general x3, matrix products, across_rows(): lax.dot_general(left, right, (((0,), (0,)), ((), ())), preferred_element_...  19.9 us
    all_to_all x1, waiting for transfers between devices, per_device(): lax.all_to_all(d_qkv_heads, 'head', split_axis=0, concat_axis=2, tiled=True)  17.1 us
  transfers between devices with their start and end apart: 5, of which 3 were waited for; matrix products, arithmetic and copies ran while one was open for 12% of the time, Pallas kernels for 0%

commit v1 on v0

v1 whole, which is shorter than its diff:
```python
import functools
import math

import jax
import jax.numpy as jnp
from jax import lax
from jax.experimental import pallas as pl
from jax.experimental.pallas import tpu as pltpu
from jax.sharding import PartitionSpec as P

F32 = jnp.float32
BF16 = jnp.bfloat16
EPS = 1e-06
AXES = ("seq", "head")
BLOCKS = 16
EXCLUDE = 32768.0
SCORE_SCALE = 0.125 * math.log2(math.e)


def dot_nn(a, b):
    return lax.dot_general(a, b, (((1,), (0,)), ((), ())), preferred_element_type=F32)


def dot_nt(a, b):
    return lax.dot_general(a, b, (((1,), (1,)), ((), ())), preferred_element_type=F32)


def dot_tn(a, b):
    return lax.dot_general(a, b, (((0,), (0,)), ((), ())), preferred_element_type=F32)


def prep_body(ids_ref, image_ref, cot_ref, gain_ref, out_ref):
    tokens, width = image_ref.shape
    step = 64
    for r in range(0, tokens, step):
        x = image_ref[r : r + step, :].astype(F32)
        center = x - jnp.mean(x, axis=-1, keepdims=True)
        spread = jnp.mean(center * center, axis=-1, keepdims=True)
        out_ref[r : r + step, 0:width] = (center * lax.rsqrt(spread + EPS) * gain_ref[...]).astype(BF16)
    out_ref[:, width : 2 * width] = cot_ref[...]
    ids = ids_ref[...]
    image = lax.broadcasted_iota(jnp.int32, (128, tokens), 0) & 63
    marks = jnp.where(image == ids, 1.0, 0.0).astype(F32)
    out_ref[:, 2 * width :] = jnp.transpose(marks).astype(BF16)


def prep(ids, image_in, cotangent, ln_gain):
    tokens, width = image_in.shape
    return pl.pallas_call(
        prep_body,
        out_shape=jax.ShapeDtypeStruct((tokens, 2 * width + 128), BF16),
        cost_estimate=pl.CostEstimate(flops=10 * tokens * width, bytes_accessed=8 * tokens * width, transcendentals=0),
        name="prep",
    )(ids, image_in, cotangent, ln_gain)


def mlp_body(pos_ref, normed_ref, cot_ref, win_ref, wout_ref, grads_ref, bo_ref, dn_ref, up_s, dact_s, act_s, dup_s):
    tokens, width = normed_ref.shape
    sid = pos_ref[1]
    up_s[...] = dot_nn(normed_ref[...], win_ref[...])
    dact_s[...] = dot_nt(cot_ref[...], wout_ref[...])
    step = 32

    def gelu_rows(i, carry):
        rows = pl.ds(pl.multiple_of(i * step, step), step)
        up = up_s[rows, :]
        cdf = 0.5 * (1.0 + lax.erf(up * math.sqrt(0.5)))
        pdf = jnp.exp(-0.5 * up * up) * (1.0 / math.sqrt(2.0 * math.pi))
        act_s[rows, :] = (up * cdf).astype(BF16)
        dup_s[rows, :] = (dact_s[rows, :] * (cdf + up * pdf)).astype(BF16)
        return carry

    lax.fori_loop(0, tokens // step, gelu_rows, 0)
    rows = width // BLOCKS
    part = 384
    for j in range(0, width, part):
        grad_out = dot_tn(act_s[:, j : j + part], cot_ref[...])
        grad_in = dot_tn(normed_ref[:, j : j + part], dup_s[...])
        for i in range(part // rows):
            where = (j // rows + i) ^ sid
            grads_ref[0, where, 0:rows, :] = grad_out[i * rows : (i + 1) * rows].astype(BF16)
            grads_ref[0, where, rows : 2 * rows, :] = grad_in[i * rows : (i + 1) * rows].astype(BF16)
    first = pl.program_id(0) == 0
    bo = dot_nn(act_s[...], wout_ref[...])
    dn = dot_nt(dup_s[...], win_ref[...])

    @pl.when(first)
    def _():
        bo_ref[...] = bo
        dn_ref[...] = dn

    @pl.when(jnp.logical_not(first))
    def _():
        bo_ref[...] += bo
        dn_ref[...] += dn


def mlp(pos, packed, w_in, w_mlp_out, part):
    tokens = packed.shape[0]
    width = w_mlp_out.shape[1]
    rows = width // BLOCKS
    first = 3 + 2 * part
    return pl.pallas_call(
        mlp_body,
        out_shape=(
            jax.ShapeDtypeStruct((2, BLOCKS, 2 * rows, width), BF16),
            jax.ShapeDtypeStruct((tokens, width), F32),
            jax.ShapeDtypeStruct((tokens, width), F32),
        ),
        grid_spec=pltpu.PrefetchScalarGridSpec(
            num_scalar_prefetch=1,
            grid=(2,),
            in_specs=[
                pl.BlockSpec((tokens, width), lambda t, pos: (0, 0)),
                pl.BlockSpec((tokens, width), lambda t, pos: (0, 1)),
                pl.BlockSpec((width, width), lambda t, pos: (0, first + t)),
                pl.BlockSpec((width, width), lambda t, pos: (2 * part + t, 0)),
            ],
            out_specs=[
                pl.BlockSpec((1, BLOCKS, 2 * rows, width), lambda t, pos: (t ^ pos[0], 0, 0, 0)),
                pl.BlockSpec((tokens, width), lambda t, pos: (0, 0)),
                pl.BlockSpec((tokens, width), lambda t, pos: (0, 0)),
            ],
            scratch_shapes=[
                pltpu.VMEM((tokens, width), F32),
                pltpu.VMEM((tokens, width), F32),
                pltpu.VMEM((tokens, width), BF16),
                pltpu.VMEM((tokens, width), BF16),
            ],
        ),
        compiler_params=pltpu.CompilerParams(dimension_semantics=("arbitrary",)),
        cost_estimate=pl.CostEstimate(
            flops=2 * 6 * 2 * tokens * width * width, bytes_accessed=16 * width * width, transcendentals=4 * tokens * width
        ),
        name=f"mlp{part}",
    )(pos, packed, packed, w_in, w_mlp_out)


def half_sums(x, low):
    left = jnp.sum(jnp.where(low, x, 0.0), axis=-1, keepdims=True)
    right = jnp.sum(jnp.where(low, 0.0, x), axis=-1, keepdims=True)
    return jnp.where(low, left, right)


def head_norm(x, low, size):
    center = x - half_sums(x, low) * (1.0 / size)
    rstd = lax.rsqrt(half_sums(center * center, low) * (1.0 / size) + EPS)
    return center * rstd, rstd


def attention_body(
    pos_ref, own_ref, mate_ref, wq_ref, wk_ref, wv_ref, wo_ref, gq_ref, gk_ref,
    grads_ref, gains_ref, part_ref,
    w_s, raw_s, dout_s, q_s, k_s, v_s, dq_s, dk_s, dv_s, att_s, dproj_s, bo_s, dn_s,
):
    tokens = own_ref.shape[0]
    width = wo_ref.shape[1]
    group = 2 * tokens
    size = 64
    pair = pl.program_id(0)
    sid = pos_ref[1]
    w_s[:, 0:128] = wq_ref[...]
    w_s[:, 128:256] = wk_ref[...]
    w_s[:, 256:384] = wv_ref[...]
    halves = ((0, own_ref), (tokens, mate_ref))
    for r, ref in halves:
        raw_s[r : r + tokens, :] = dot_nn(ref[:, 0:width], w_s[...]).astype(BF16)
        dout_s[r : r + tokens, :] = dot_nt(ref[:, width : 2 * width], wo_ref[...]).astype(BF16)

    step = 128

    def lanes(rows):
        return lax.broadcasted_iota(jnp.int32, (rows, 128), 1)

    for r, ref in halves:

        def norm_rows(i, carry, r=r, ref=ref):
            here = pl.ds(pl.multiple_of(i * step, step), step)
            rows = pl.ds(pl.multiple_of(r + i * step, step), step)
            low = lanes(step) < size
            marks = ref[here, 2 * width :].astype(F32)
            qn = head_norm(raw_s[rows, 0:128].astype(F32), low, size)[0] * gq_ref[...]
            kn = head_norm(raw_s[rows, 128:256].astype(F32), low, size)[0] * gk_ref[...]
            v = raw_s[rows, 256:384].astype(F32)
            away = (marks - 1.0) * EXCLUDE
            for h in range(2):
                mine = low if h == 0 else jnp.logical_not(low)
                q_s[h, rows, :] = jnp.where(mine, qn, marks).astype(BF16)
                k_s[h, rows, :] = jnp.where(mine, kn, away).astype(BF16)
                v_s[h, rows, :] = jnp.where(mine, v, 1.0).astype(BF16)
            return carry

        lax.fori_loop(0, tokens // step, norm_rows, 0)

    block = 256
    dk_s[...] = jnp.zeros_like(dk_s)
    dv_s[...] = jnp.zeros_like(dv_s)

    def query_block(i, carry):
        rows = pl.ds(pl.multiple_of(i * block, block), block)
        lane = lanes(block)
        low = lane < size
        for h in range(2):
            mine = low if h == 0 else jnp.logical_not(low)
            spare = size if h == 0 else 0
            q = q_s[h, rows, :]
            expd = jnp.exp2(dot_nt(q, k_s[h]) * SCORE_SCALE)
            expd_low = expd.astype(BF16)
            outs = dot_nn(expd_low, v_s[h])
            inverse = 1.0 / pltpu.roll(outs, size, 1)
            attended = outs * inverse
            grad = dout_s[rows, :].astype(F32) * inverse
            grad_low = grad.astype(BF16).astype(F32)
            centre = jnp.sum(jnp.where(mine, grad_low * attended, 0.0), axis=-1, keepdims=True)
            centre_high = centre.astype(BF16).astype(F32)
            extra = jnp.where(lane == spare, -centre_high, jnp.where(lane == spare + 1, centre_high - centre, 0.0))
            grad_ext = jnp.where(mine, grad_low, extra).astype(BF16)
            d_scores = (expd * dot_nt(grad_ext, v_s[h])).astype(BF16)
            dv_s[h] += dot_tn(expd_low, grad_ext)
            dk_s[h] += dot_tn(d_scores, q)
            dq = dot_nn(d_scores, k_s[h])
            if h == 0:
                att_s[rows, :] = attended
                dq_s[rows, :] = dq
            else:
                att_s[rows, :] = jnp.where(mine, attended, att_s[rows, :])
                dq_s[rows, :] = jnp.where(mine, dq, dq_s[rows, :])
        return carry

    lax.fori_loop(0, group // block, query_block, 0)

    @pl.when(pair == 0)
    def _():
        gains_ref[...] = jnp.zeros_like(gains_ref)

    def norm_back(i, carry):
        rows = pl.ds(pl.multiple_of(i * step, step), step)
        low = lanes(step) < size
        grads = (dq_s[rows, :], jnp.where(low, dk_s[0, rows, :], dk_s[1, rows, :]))
        for n, (grad, gain_ref) in enumerate(zip(grads, (gq_ref, gk_ref))):
            scaled, rstd = head_norm(raw_s[rows, 128 * n : 128 * (n + 1)].astype(F32), low, size)
            grad = grad * 0.125
            gains_ref[8 * n : 8 * (n + 1), :] += jnp.sum((grad * scaled).reshape(step // 8, 8, 128), axis=0)
            grad = grad * gain_ref[...]
            mean = half_sums(grad, low) * (1.0 / size)
            slope = half_sums(grad * scaled, low) * (1.0 / size)
            dproj_s[rows, 128 * n : 128 * (n + 1)] = (rstd * (grad - mean - scaled * slope)).astype(BF16)
        dproj_s[rows, 256:384] = jnp.where(low, dv_s[0, rows, :], dv_s[1, rows, :]).astype(BF16)
        return carry

    lax.fori_loop(0, group // step, norm_back, 0)

    rows = width // BLOCKS
    part = 384
    for j in range(0, width, part):
        grad_in = dot_tn(own_ref[:, j : j + part], dproj_s[0:tokens, :])
        grad_in += dot_tn(mate_ref[:, j : j + part], dproj_s[tokens:group, :])
        for i in range(part // rows):
            grads_ref[(j // rows + i) ^ sid, 0:rows, :] = grad_in[i * rows : (i + 1) * rows].astype(BF16)
    grad_out = dot_tn(att_s[0:tokens, :].astype(BF16), own_ref[:, width : 2 * width])
    grad_out += dot_tn(att_s[tokens:group, :].astype(BF16), mate_ref[:, width : 2 * width])
    few = 128 // BLOCKS
    for i in range(BLOCKS):
        piece = grad_out[i * few : (i + 1) * few]
        piece = jnp.concatenate([piece[:, :384], piece[:, 384:]], axis=0)
        grads_ref[i ^ sid, rows : rows + 2 * few, :] = piece.astype(BF16)

    bo = dot_nn(att_s[...].astype(BF16), wo_ref[...])
    dn = dot_nt(dproj_s[...], w_s[...])

    @pl.when(pair == 0)
    def _():
        bo_s[...] = bo
        dn_s[...] = dn

    @pl.when(pair == 1)
    def _():
        bo_s[...] += bo
        dn_s[...] += dn

    @pl.when(pair == 2)
    def _():
        for n in range(2):
            there = slice(n * tokens, (n + 1) * tokens)
            part_ref[n, :, 0:width] = (bo_s[there, :] + bo[there, :]).astype(BF16)
            part_ref[n, :, width : 2 * width] = (dn_s[there, :] + dn[there, :]).astype(BF16)


def attention(pos, own, mate, w_in, w_attn_out, gain_q, gain_k):
    tokens, packed = own.shape
    width = w_attn_out.shape[1]
    group = 2 * tokens
    rows = width // BLOCKS + 16
    whole = pl.BlockSpec((tokens, packed), lambda p, pos: (0, 0))
    gain = pl.BlockSpec((1, 128), lambda p, pos: (0, 0))
    return pl.pallas_call(
        attention_body,
        out_shape=(
            jax.ShapeDtypeStruct((BLOCKS, rows, 3 * 384), BF16),
            jax.ShapeDtypeStruct((16, 128), F32),
            jax.ShapeDtypeStruct((2, tokens, 2 * width), BF16),
        ),
        grid_spec=pltpu.PrefetchScalarGridSpec(
            num_scalar_prefetch=1,
            grid=(3,),
            in_specs=[
                whole,
                whole,
                pl.BlockSpec((width, 128), lambda p, pos: (0, 3 * pos[0] + p)),
                pl.BlockSpec((width, 128), lambda p, pos: (0, 6 + 3 * pos[0] + p)),
                pl.BlockSpec((width, 128), lambda p, pos: (0, 12 + 3 * pos[0] + p)),
                pl.BlockSpec((128, width), lambda p, pos: (3 * pos[0] + p, 0)),
                gain,
                gain,
            ],
            out_specs=[
                pl.BlockSpec((BLOCKS, rows, 384), lambda p, pos: (0, 0, p)),
                pl.BlockSpec((16, 128), lambda p, pos: (0, 0)),
                pl.BlockSpec((2, tokens, 2 * width), lambda p, pos: (0, 0, 0)),
            ],
            scratch_shapes=[
                pltpu.VMEM((width, 384), BF16),
                pltpu.VMEM((group, 384), BF16),
                pltpu.VMEM((group, 128), BF16),
                pltpu.VMEM((2, group, 128), BF16),
                pltpu.VMEM((2, group, 128), BF16),
                pltpu.VMEM((2, group, 128), BF16),
                pltpu.VMEM((group, 128), F32),
                pltpu.VMEM((2, group, 128), F32),
                pltpu.VMEM((2, group, 128), F32),
                pltpu.VMEM((group, 128), F32),
                pltpu.VMEM((group, 384), BF16),
                pltpu.VMEM((group, width), F32),
                pltpu.VMEM((group, width), F32),
            ],
        ),
        compiler_params=pltpu.CompilerParams(dimension_semantics=("arbitrary",)),
        cost_estimate=pl.CostEstimate(
            flops=6 * 6 * 2 * group * group * 128, bytes_accessed=16 * tokens * width, transcendentals=6 * group * group
        ),
        name="attention",
    )(pos, own, mate, w_in, w_in, w_in, w_attn_out, gain_q, gain_k)


def finish_body(image_ref, cot_ref, gain_ref, bo_ref, dn_ref, bo2_ref, dn2_ref, got_ref, out_ref, grad_ref, ln_ref):
    tokens, width = image_ref.shape
    step = 32
    ln_ref[...] = jnp.zeros_like(ln_ref)

    def some_rows(i, carry):
        rows = pl.ds(pl.multiple_of(i * step, step), step)
        x = image_ref[rows, :].astype(F32)
        got = got_ref[rows, :].astype(F32)
        out_ref[rows, :] = (x + (bo_ref[rows, :] + bo2_ref[rows, :] + got[:, 0:width])).astype(BF16)
        center = x - jnp.mean(x, axis=-1, keepdims=True)
        rstd = lax.rsqrt(jnp.mean(center * center, axis=-1, keepdims=True) + EPS)
        scaled = center * rstd
        grad = dn_ref[rows, :] + dn2_ref[rows, :] + got[:, width : 2 * width]
        ln_ref[...] += jnp.sum((grad * scaled).reshape(step // 8, 8, width), axis=0)
        grad = grad * gain_ref[...]
        mean = jnp.mean(grad, axis=-1, keepdims=True)
        slope = jnp.mean(grad * scaled, axis=-1, keepdims=True)
        grad_ref[rows, :] = cot_ref[rows, :].astype(F32) + rstd * (grad - mean - scaled * slope)
        return carry

    lax.fori_loop(0, tokens // step, some_rows, 0)


def finish(image_in, cotangent, ln_gain, bo, dn, bo2, dn2, got):
    tokens, width = image_in.shape
    return pl.pallas_call(
        finish_body,
        out_shape=(
            jax.ShapeDtypeStruct((tokens, width), BF16),
            jax.ShapeDtypeStruct((tokens, width), F32),
            jax.ShapeDtypeStruct((8, width), F32),
        ),
        cost_estimate=pl.CostEstimate(flops=30 * tokens * width, bytes_accessed=30 * tokens * width, transcendentals=0),
        name="finish",
    )(image_in, cotangent, ln_gain, bo, dn, bo2, dn2, got)


def exchange(value, mask):
    count = lax.axis_size(AXES)
    return lax.ppermute(value, AXES, [(i, i ^ mask) for i in range(count)])


def add_low(left, right):
    return (left.astype(F32) + right.astype(F32)).astype(BF16)


def reduce_scatter(chunk, masks, rest):
    for mask in masks:
        half = chunk.shape[0] // 2
        chunk = add_low(chunk[:half], exchange(chunk[half:], mask))
    for mask in rest:
        chunk = add_low(chunk, exchange(chunk, mask))
    return chunk


def all_gather(chunk, masks):
    for mask in reversed(masks):
        chunk = jnp.concatenate([chunk, exchange(chunk, mask)], axis=0)
    return chunk


def spread_mlp_body(pos_ref, own_ref, mate_ref, *refs):
    out_ref, in_ref = refs[-2:]
    sid = pos_ref[1]
    rows = own_ref.shape[1] // 2
    side, quarter = pl.program_id(0), pl.program_id(1)

    def put(source):
        for i in range(4):
            at = (4 * quarter + i) ^ sid
            out_ref[i * rows : (i + 1) * rows, :] = source[at, 0:rows, :].astype(F32)
            in_ref[i * rows : (i + 1) * rows, :] = source[at, rows : 2 * rows, :].astype(F32)

    pl.when(side == 0)(lambda: put(own_ref))
    pl.when(side == 1)(lambda: put(mate_ref))


def spread_mlp(pos, own, mate, part, shapes, before):
    blocks, rows2, width = own.shape
    whole = pl.BlockSpec(own.shape, lambda r, g, pos: (0, 0, 0))
    return pl.pallas_call(
        spread_mlp_body,
        out_shape=tuple(jax.ShapeDtypeStruct(s, F32) for s in shapes),
        grid_spec=pltpu.PrefetchScalarGridSpec(
            num_scalar_prefetch=1,
            grid=(2, 4),
            in_specs=[whole, whole] + [pl.BlockSpec(memory_space=pl.ANY)] * len(before),
            out_specs=[
                pl.BlockSpec((width // 4, width), lambda r, g, pos: (4 * (2 * part + (r ^ pos[0])) + g, 0)),
                pl.BlockSpec((width // 4, width), lambda r, g, pos: (g, 3 + 2 * part + (r ^ pos[0]))),
            ],
        ),
        input_output_aliases={3 + i: i for i in range(len(before))},
        compiler_params=pltpu.CompilerParams(dimension_semantics=("arbitrary", "arbitrary")),
        cost_estimate=pl.CostEstimate(flops=0, bytes_accessed=24 * width * width, transcendentals=0),
        name=f"spread_mlp{part}",
    )(pos, own, mate, *before)


def spread_attention_body(pos_ref, own_ref, mate_ref, _, in_ref, out_ref):
    sid = pos_ref[1]
    blocks = own_ref.shape[0]
    rows = own_ref.shape[1] - 16
    side, kind = pl.program_id(0), pl.program_id(1)

    def put(source):
        for i in range(blocks):
            at = i ^ sid
            for p in range(3):
                from_col = pl.ds(pl.multiple_of(384 * p + 128 * kind, 128), 128)
                in_ref[i * rows : (i + 1) * rows, 128 * p : 128 * (p + 1)] = source[at, 0:rows, from_col].astype(F32)

        @pl.when(kind == 0)
        def _():
            for i in range(blocks):
                at = i ^ sid
                for p in range(3):
                    piece = source[at, rows : rows + 16, 384 * p : 384 * (p + 1)].astype(F32)
                    to = slice(128 * p + 8 * i, 128 * p + 8 * (i + 1))
                    out_ref[to, 0:384] = piece[0:8]
                    out_ref[to, 384:768] = piece[8:16]

    pl.when(side == 0)(lambda: put(own_ref))
    pl.when(side == 1)(lambda: put(mate_ref))


def spread_attention(pos, own, mate, before, out_shape):
    whole = pl.BlockSpec(own.shape, lambda r, k, pos: (0, 0, 0))
    width = out_shape[0]
    return pl.pallas_call(
        spread_attention_body,
        out_shape=(jax.ShapeDtypeStruct(before.shape, F32), jax.ShapeDtypeStruct(out_shape, F32)),
        grid_spec=pltpu.PrefetchScalarGridSpec(
            num_scalar_prefetch=1,
            grid=(2, 3),
            in_specs=[whole, whole, pl.BlockSpec(memory_space=pl.ANY)],
            out_specs=[
                pl.BlockSpec((width, 384), lambda r, k, pos: (0, 2 * k + (r ^ pos[0]))),
                pl.BlockSpec((384, width), lambda r, k, pos: (r ^ pos[0], 0)),
            ],
        ),
        input_output_aliases={3: 0},
        compiler_params=pltpu.CompilerParams(dimension_semantics=("arbitrary", "arbitrary")),
        cost_estimate=pl.CostEstimate(flops=0, bytes_accessed=24 * width * width, transcendentals=0),
        name="spread_attention",
    )(pos, own, mate, before)


def per_device(image_in, ln_gain, w_in, q_gain, k_gain, w_attn_out, w_mlp_out, cotangent, image_ids):
    tokens, width = image_in.shape
    count = lax.axis_size(AXES)
    index = lax.axis_index(AXES)
    side = index & 1
    core = (index >> 1) & 1
    others = [1 << k for k in range(2, count.bit_length() - 1)]
    masks_x = [1] + others[:3]
    masks_y = [others[0], 1] + others[1:3]
    rest = others[3:]

    def place(masks):
        sid = jnp.int32(0)
        for mask in masks:
            sid = 2 * sid + ((index & mask) != 0).astype(jnp.int32)
        return jnp.stack([core, sid])

    pos_x, pos_y = place(masks_x), place(masks_y)
    gain_row = ln_gain.reshape(1, width)
    ids = lax.dynamic_slice(image_ids, (0, side * tokens), (1, tokens))
    packed = prep(ids, image_in, cotangent, gain_row)
    swapped = lax.ppermute(
        packed, AXES, [(i, (i & ~3) | ((i & 1) << 1) | ((i >> 1) & 1)) for i in range(count)]
    )
    grads0, bo0, dn0 = mlp(pos_x, packed, w_in, w_mlp_out, 0)
    mate = exchange(swapped, 2)
    grads1, bo1, dn1 = mlp(pos_y, packed, w_in, w_mlp_out, 1)

    def gather(chunk, masks):
        shard = reduce_scatter(chunk, masks, rest)
        own = all_gather(shard, masks)
        return own, exchange(own, 2)

    def pair_sum(grads):
        return add_low(grads[0], exchange(grads[1], 2))

    own0, mate0 = gather(pair_sum(grads0), masks_x)
    own1, mate1 = gather(pair_sum(grads1), masks_y)
    gain_q = jnp.concatenate([q_gain, q_gain]).reshape(1, 128)
    gain_k = jnp.concatenate([k_gain, k_gain]).reshape(1, 128)
    grads2, gains, parts = attention(pos_x, swapped, mate, w_in, w_attn_out, gain_q, gain_k)
    joined = add_low(parts[0], exchange(parts[1], 2))
    got = lax.ppermute(
        joined, AXES, [(i, (i & ~3) | ((i & 1) << 1) | ((i >> 1) & 1)) for i in range(count)]
    )
    own2, mate2 = gather(grads2, masks_x)
    block_out, grad_image, ln_part = finish(image_in, cotangent, gain_row, bo0, dn0, bo1, dn1, got)
    ln_row = jnp.sum(ln_part, axis=0)
    gain_rows = jnp.sum(gains.reshape(2, 8, 2, 64), axis=(1, 2))
    small = jnp.concatenate([ln_row, gain_rows.reshape(128), jnp.zeros((128,), F32)]).reshape(1, 8, 128)
    small = lax.all_to_all(jnp.broadcast_to(small, (count, 8, 128)), AXES, split_axis=0, concat_axis=0, tiled=True)
    small = jnp.sum(small, axis=0).reshape(1024)
    shapes = (w_mlp_out.shape, w_in.shape)
    grad_mlp_w, grad_win = spread_mlp(pos_x, own0, mate0, 0, shapes, ())
    grad_mlp_w, grad_win = spread_mlp(pos_y, own1, mate1, 1, shapes, (grad_mlp_w, grad_win))
    grad_win, grad_attn_w = spread_attention(pos_x, own2, mate2, grad_win, w_attn_out.shape)
    return (
        block_out, grad_image, small[0:width], grad_win, small[width : width + 64],
        small[width + 64 : width + 128], grad_attn_w, grad_mlp_w,
    )


def solution(mesh):
    tokens = P(("seq", "head"), None)
    return jax.shard_map(
        per_device,
        mesh=mesh,
        in_specs=(tokens, P(), P(), P(), P(), P(), P(), tokens, P("seq", None)),
        out_specs=(tokens, tokens, P(), P(), P(), P(), P(), P()),
        check_vma=False,
    )
```

time: 782 us -> 370 us (0.47)
  waiting for transfers between devices: 391 us -> 112 us
  Pallas kernels: 0 us -> 136 us
  matrix products: 117 us -> 0 us
  local copies, waits for them, and re-layouts: 127 us -> 19.4 us
  starting transfers between devices: 19.4 us -> 71.2 us
  other arithmetic: 62.5 us -> 12.4 us
  blocking collectives: 41.6 us -> 15.2 us
  between operations: 15 us -> 1.08 us
    psum x1 -> x0, waiting for transfers between devices: 368 us -> none  [per_device(): lax.psum((grad_win, grad_attn_w, grad_mlp_w, grad_lng, grad_qg, grad_kg),...]
    pallas_call x0 -> x8, Pallas kernels: none -> 136 us  [the longest x1 68.2 us: attention(): pl.pallas_call(attention_body, out_shape=(jax.ShapeDtypeStruct((BLOCKS, r...]
    dot_general x23 -> x0, matrix products: 117 us -> none  [the longest x3 29.3 us: against_cols(): lax.dot_general(left, right, (((1,), (1,)), ((), ())), preferred_element_...]
    ppermute x0 -> x33, waiting for transfers between devices: none -> 112 us  [the longest x31 112 us: exchange(): return lax.ppermute(value, AXES, [(i, i ^ mask) for i in range(count)])]
    ppermute x0 -> x33, starting transfers between devices: none -> 71.2 us  [the longest x31 43.8 us: exchange(): return lax.ppermute(value, AXES, [(i, i ^ mask) for i in range(count)])]
    psum x1 -> x0, blocking collectives: 41.6 us -> none  [per_device(): lax.psum((grad_win, grad_attn_w, grad_mlp_w, grad_lng, grad_qg, grad_kg),...]
    dynamic_update_slice x4 -> x0, local copies, waits for them, and re-layouts: 33.3 us -> none  [per_device(): out_blocks, log_total = lax.map(forward_block, (query_blocks, id_blocks))]
    unnamed x101 -> x35, local copies, waits for them, and re-layouts: 32.1 us -> 6.11 us
  transfers between devices with their start and end apart: 5 -> 33, of which waited for: 3 -> 13; matrix products, arithmetic and copies ran while one was open for 12% -> 8% of each run, Pallas kernels for 0% -> 34%
where the time goes in v1:
time: 370 us; the launch traced here: 368 us
  Pallas kernels  136 us (37%)
  waiting for transfers between devices  112 us (30%)
  starting transfers between devices  71.2 us (19%)
  local copies, waits for them, and re-layouts  19.4 us (5%)
  blocking collectives  15.2 us (4%)
  other arithmetic  12.4 us (3%)
    ppermute x31, waiting for transfers between devices, exchange(): return lax.ppermute(value, AXES, [(i, i ^ mask) for i in range(count)])  112 us
    pallas_call x1, Pallas kernels, attention(): pl.pallas_call(attention_body, out_shape=(jax.ShapeDtypeStruct((BLOCKS, r...  68.2 us
    ppermute x31, starting transfers between devices, exchange(): return lax.ppermute(value, AXES, [(i, i ^ mask) for i in range(count)])  43.8 us
    pallas_call x2, Pallas kernels, mlp(): pl.pallas_call(mlp_body, out_shape=(jax.ShapeDtypeStruct((2, BLOCKS, 2 *...  31.1 us
    pallas_call x2, Pallas kernels, spread_mlp(): pl.pallas_call(spread_mlp_body, out_shape=tuple((jax.ShapeDtypeStruct(s,...  15.6 us
    all_to_all x1, blocking collectives, per_device(): lax.all_to_all(jnp.broadcast_to(small, (count, 8, 128)), AXES, split_axis...  15.2 us
    ppermute x1, starting transfers between devices, per_device(): lax.ppermute(packed, AXES, [(i, i & ~3 | (i & 1) << 1 | i >> 1 & 1) for i...  14.2 us
    ppermute x1, starting transfers between devices, per_device(): lax.ppermute(joined, AXES, [(i, i & ~3 | (i & 1) << 1 | i >> 1 & 1) for i...  13.3 us
  transfers between devices with their start and end apart: 33, of which 13 were waited for; matrix products, arithmetic and copies ran while one was open for 8% of the time, Pallas kernels for 34%

profile of v1, /device:TPU:0, one launch (start us, length us, event | category | flops | bytes accessed | tf_op | source)
XLA Modules:
  0.0 367.6 jit_solution(13276928898650945743)
XLA Ops:
  2.5 3.2 prep.1.normed_ref.cot_ref
  5.7 14.2 %collective-permute-start = (bf16[512,1664]{1,0:T(8,128)(2,1)}, bf16[512,1664]{1,0:T(8,128)(2,1)}, u32[]{:S(2)}, u32[]{:S(2)}) collective-permute-start(bf16[512,1664]{1,0:T(8,128)(2,1)} %prep.1.normed_ref.cot_ref), channel_id=1, source_target_pairs={{0,0},{1,2},{2,1},{3,3},{4,4},{5,6},{6,5},{7,7},{8,8},{9,10},{10,9... | collective-permute-start | bytes 5111816 | tf_op jit(solution)/shard_map/ppermute | solution.py:515
  20.6 15.5 %mlp1.1 = (bf16[2,16,96,768]{3,2,1,0:T(8,128)(2,1)}, f32[512,768]{1,0:T(8,128)}, f32[512,768]{1,0:T(8,128)}) custom-call(s32[2]{0:T(128)} %pad_add_fusion.1.pos_ref, bf16[512,1664]{1,0:T(8,128)(2,1)} %prep.1.normed_ref.cot_ref, bf16[512,1664]{1,0:T(8,128)(2,1)} %prep.1.normed_ref.cot_ref, bf16[768,5376]{1,0:T(8,128)(2,1)} %wv_ref.1, bf16[3072,768]{1,0:T(8,128)(2,1)} %wout_ref.3), custom_call_target="tpu_custom_call" | custom-call | flops 7247757312 | bytes 9437184 | tf_op jit(solution)/shard_map/mlp1/pallas_call | solution.py:103
  38.6 15.6 %mlp0.1 = (bf16[2,16,96,768]{3,2,1,0:T(8,128)(2,1)}, f32[512,768]{1,0:T(8,128)}, f32[512,768]{1,0:T(8,128)}) custom-call(s32[2]{0:T(128)} %pad_add_fusion.pos_ref, bf16[512,1664]{1,0:T(8,128)(2,1)} %prep.1.normed_ref.cot_ref, bf16[512,1664]{1,0:T(8,128)(2,1)} %prep.1.normed_ref.cot_ref, bf16[768,5376]{1,0:T(8,128)(2,1)} %wv_ref.1, bf16[3072,768]{1,0:T(8,128)(2,1)} %wout_ref.3), custom_call_target="tpu_custom_call" | custom-call | flops 7247757312 | bytes 9437184 | tf_op jit(solution)/shard_map/mlp0/pallas_call | solution.py:103
  68.7 68.2 %attention.1 = (bf16[16,64,1152]{2,1,0:T(8,128)(2,1)}, f32[16,128]{1,0:T(8,128)}, bf16[2,512,1536]{2,1,0:T(8,128)(2,1)}) custom-call(s32[2]{0:T(128)} %pad_add_fusion.pos_ref, bf16[512,1664]{1,0:T(8,128)(2,1)} %collective-permute-done.own_ref, bf16[512,1664]{1,0:T(8,128)(2,1)} %collective-permute-done.1.mate_ref, bf16[768,5376]{1,0:T(8,128)(2,1)} %wv_ref.1, ...), custom_call_target="tpu_custom_call" | custom-call | flops 9663676416 | bytes 6291456 | tf_op jit(solution)/shard_map/attention/pallas_call | solution.py:296
  142.9 35.4 %collective-permute-done.15 = bf16[4,96,768]{2,1,0:T(8,128)(2,1)S(1)} collective-permute-done((bf16[4,96,768]{2,1,0:T(8,128)(2,1)S(1)}, bf16[4,96,768]{2,1,0:T(8,128)(2,1)S(1)}, u32[]{:S(2)}, u32[]{:S(2)}) %collective-permute-start.15) | collective-permute-done | bytes 589856 | tf_op jit(solution)/shard_map/ppermute | solution.py:385
  182.4 5.2 %collective-permute-done.16 = bf16[2,96,768]{2,1,0:T(8,128)(2,1)S(1)} collective-permute-done((bf16[2,96,768]{2,1,0:T(8,128)(2,1)S(1)}, bf16[2,96,768]{2,1,0:T(8,128)(2,1)S(1)}, u32[]{:S(2)}, u32[]{:S(2)}) %collective-permute-start.16) | collective-permute-done | bytes 294944 | tf_op jit(solution)/shard_map/ppermute | solution.py:385
  187.6 3.9 %collective-permute-start.17 = (bf16[1,96,768]{2,1,0:T(8,128)(2,1)S(1)}, bf16[1,96,768]{2,1,0:T(8,128)(2,1)S(1)}, u32[]{:S(2)}, u32[]{:S(2)}) collective-permute-start(bf16[1,96,768]{2,1,0:T(8,128)(2,1)S(1)} %slice.149), channel_id=1, source_target_pairs={{0,16},{1,17},{2,18},{3,19},{4,20},{5,21},{6,22},{7,23},{8,24},{9,... | collective-permute-start | bytes 442376 | tf_op jit(solution)/shard_map/ppermute | solution.py:385
  200.9 7.2 %collective-permute-done.6 = bf16[2,64,1152]{2,1,0:T(8,128)(2,1)S(1)} collective-permute-done((bf16[2,64,1152]{2,1,0:T(8,128)(2,1)S(1)}, bf16[2,64,1152]{2,1,0:T(8,128)(2,1)S(1)}, u32[]{:S(2)}, u32[]{:S(2)}) %collective-permute-start.6) | collective-permute-done | bytes 294944 | tf_op jit(solution)/shard_map/ppermute | solution.py:385
  211.9 3.5 collective-permute-done.18
  215.4 3.9 %collective-permute-start.19 = (bf16[2,96,768]{2,1,0:T(8,128)(2,1)S(1)}, bf16[2,96,768]{2,1,0:T(8,128)(2,1)S(1)}, u32[]{:S(2)}, u32[]{:S(2)}) collective-permute-start(bf16[2,96,768]{2,1,0:T(8,128)(2,1)S(1)} %pad_maximum_fusion.7), channel_id=1, source_target_pairs={{0,8},{1,9},{2,10},{3,11},{4,12},{5,13},{6,14},{7,15},{8,0},{9,1},... | collective-permute-start | bytes 884744 | tf_op jit(solution)/shard_map/ppermute | solution.py:385
  219.3 3.4 collective-permute-start.8
  225.0 3.6 collective-permute-start.29
  229.3 3.0 collective-permute-start.9
  245.3 13.3 %collective-permute-start.3 = (bf16[512,1536]{1,0:T(8,128)(2,1)}, bf16[512,1536]{1,0:T(8,128)(2,1)}, u32[]{:S(2)}, u32[]{:S(2)}) collective-permute-start(bf16[512,1536]{1,0:T(8,128)(2,1)} %fusion.2), channel_id=1, source_target_pairs={{0,0},{1,2},{2,1},{3,3},{4,4},{5,6},{6,5},{7,7},{8,8},{9,10},{10,9... | collective-permute-start | bytes 4718600 | tf_op jit(solution)/shard_map/ppermute | solution.py:536
  260.5 5.3 %collective-permute-done.10 = bf16[4,64,1152]{2,1,0:T(8,128)(2,1)S(1)} collective-permute-done((bf16[4,64,1152]{2,1,0:T(8,128)(2,1)S(1)}, bf16[4,64,1152]{2,1,0:T(8,128)(2,1)S(1)}, u32[]{:S(2)}, u32[]{:S(2)}) %collective-permute-start.10) | collective-permute-done | bytes 589856 | tf_op jit(solution)/shard_map/ppermute | solution.py:385
  268.1 19.5 %collective-permute-done.21 = bf16[8,96,768]{2,1,0:T(8,128)(2,1)S(1)} collective-permute-done((bf16[8,96,768]{2,1,0:T(8,128)(2,1)S(1)}, bf16[8,96,768]{2,1,0:T(8,128)(2,1)S(1)}, u32[]{:S(2)}, u32[]{:S(2)}) %collective-permute-start.21) | collective-permute-done | bytes 1179680 | tf_op jit(solution)/shard_map/ppermute | solution.py:385
  288.6 7.3 %collective-permute-done.31 = bf16[8,96,768]{2,1,0:T(8,128)(2,1)S(1)} collective-permute-done((bf16[8,96,768]{2,1,0:T(8,128)(2,1)S(1)}, bf16[8,96,768]{2,1,0:T(8,128)(2,1)S(1)}, u32[]{:S(2)}, u32[]{:S(2)}) %collective-permute-start.31) | collective-permute-done | bytes 1179680 | tf_op jit(solution)/shard_map/ppermute | solution.py:385
  297.1 19.5 %collective-permute-done.11 = bf16[8,64,1152]{2,1,0:T(8,128)(2,1)S(1)} collective-permute-done((bf16[8,64,1152]{2,1,0:T(8,128)(2,1)S(1)}, bf16[8,64,1152]{2,1,0:T(8,128)(2,1)S(1)}, u32[]{:S(2)}, u32[]{:S(2)}) %collective-permute-start.11) | collective-permute-done | bytes 1179680 | tf_op jit(solution)/shard_map/ppermute | solution.py:385
  317.0 10.0 %finish.1 = (bf16[512,768]{1,0:T(8,128)(2,1)}, f32[512,768]{1,0:T(8,128)}, f32[8,768]{1,0:T(8,128)}) custom-call(bf16[512,768]{1,0:T(8,128)(2,1)} %image_ref.3, bf16[512,768]{1,0:T(8,128)(2,1)} %cot_ref.3, f32[1,768]{1,0:T(1,128)} %reshape.43.gain_ref, f32[512,768]{1,0:T(8,128)} %get-tuple-element.26.bo_ref, f32[512,768]{1,0:T(8,128)} %get-tuple-element.27.dn_ref, ...), custom_call_target="tpu_custom_call" | custom-call | flops 11796480 | bytes 11796480 | tf_op jit(solution)/shard_map/finish/pallas_call | solution.py:371
  327.8 15.2 %all_to_all.5 = f32[32,8,128]{2,1,0:T(8,128)S(1)} all-to-all(f32[32,8,128]{2,1,0:T(8,128)S(1)} %broadcast_in_dim.12), channel_id=1, replica_groups=mesh['seq'=16,'head'=2] {'seq','head'}, dimensions={0} | all-to-all | bytes 262144 | tf_op jit(solution)/shard_map/all_to_all | solution.py:544
  344.2 7.8 %spread_mlp0.1 = (f32[3072,768]{1,0:T(8,128)}, f32[768,5376]{1,0:T(8,128)}) custom-call(s32[2]{0:T(128)} %pad_add_fusion.pos_ref, bf16[16,96,768]{2,1,0:T(8,128)(2,1)} %constant_dynamic-update-slice_fusion.10.own_ref, bf16[16,96,768]{2,1,0:T(8,128)(2,1)} %collective-permute-done.32.mate_ref), custom_call_target="tpu_custom_call" | custom-call | bytes 14155776 | tf_op jit(solution)/shard_map/spread_mlp0/pallas_call | solution.py:426
  352.1 7.8 %spread_mlp1.1 = (f32[3072,768]{1,0:T(8,128)}, f32[768,5376]{1,0:T(8,128)}) custom-call(s32[2]{0:T(128)} %pad_add_fusion.1.pos_ref, bf16[16,96,768]{2,1,0:T(8,128)(2,1)} %constant_dynamic-update-slice_fusion.5.own_ref, bf16[16,96,768]{2,1,0:T(8,128)(2,1)} %collective-permute-done.22.mate_ref, ...), custom_call_target="tpu_custom_call", output_to_operand_aliasing={{0}: (3, {}), {1}: (4, {})} | custom-call | bytes 14155776 | tf_op jit(solution)/shard_map/spread_mlp1/pallas_call | solution.py:426
  359.9 7.7 %spread_attention.1 = (f32[768,5376]{1,0:T(8,128)}, f32[768,768]{1,0:T(8,128)}) custom-call(s32[2]{0:T(128)} %pad_add_fusion.pos_ref, bf16[16,64,1152]{2,1,0:T(8,128)(2,1)} %copy-done.6, bf16[16,64,1152]{2,1,0:T(8,128)(2,1)} %collective-permute-done.12.mate_ref, f32[768,5376]{1,0:T(8,128)} %get-tuple-element.40._), custom_call_target="tpu_custom_call", output_to_operand_aliasing={{0}: (3, {})} | custom-call | bytes 14155776 | tf_op jit(solution)/shard_map/spread_attention/pallas_call | solution.py:475
  (144 shorter events, 67.4 us)
Async XLA Ops:
  5.7 51.0 %collective-permute-start = (bf16[512,1664]{1,0:T(8,128)(2,1)}, bf16[512,1664]{1,0:T(8,128)(2,1)}, u32[]{:S(2)}, u32[]{:S(2)}) collective-permute-start(bf16[512,1664]{1,0:T(8,128)(2,1)} %prep.1.normed_ref.cot_ref), channel_id=1, source_target_pairs={{0,0},{1,2},{2,1},{3,3},{4,4},{5,6},{6,5},{7,7},{8,8},{9,10},{10,9... | collective-permute-start | bytes 5111816 | tf_op jit(solution)/shard_map/ppermute | solution.py:515
  37.9 19.6 %collective-permute-start.13 = (bf16[16,96,768]{2,1,0:T(8,128)(2,1)S(1)}, bf16[16,96,768]{2,1,0:T(8,128)(2,1)}, u32[]{:S(2)}, u32[]{:S(2)}) collective-permute-start(bf16[16,96,768]{2,1,0:T(8,128)(2,1)S(1)} %slice_bitcast_fusion.1), channel_id=1, source_target_pairs={{0,2},{1,3},{2,0},{3,1},{4,6},{5,7},{6,4},{7,5},{8,10},{9,11},{10,... | collective-permute-start | bytes 7077896 | tf_op jit(solution)/shard_map/ppermute | solution.py:385
  61.1 78.0 %collective-permute-start.14 = (bf16[8,96,768]{2,1,0:T(8,128)(2,1)}, bf16[8,96,768]{2,1,0:T(8,128)(2,1)S(1)}, u32[]{:S(2)}, u32[]{:S(2)}) collective-permute-start(bf16[8,96,768]{2,1,0:T(8,128)(2,1)} %slice.143), channel_id=1, source_target_pairs={{0,4},{1,5},{2,6},{3,7},{4,0},{5,1},{6,2},{7,3},{8,12},{9,13},{10,... | collective-permute-start | bytes 3538952 | tf_op jit(solution)/shard_map/ppermute | solution.py:385
  67.4 73.4 %collective-permute-start.24 = (bf16[8,96,768]{2,1,0:T(8,128)(2,1)}, bf16[8,96,768]{2,1,0:T(8,128)(2,1)}, u32[]{:S(2)}, u32[]{:S(2)}) collective-permute-start(bf16[8,96,768]{2,1,0:T(8,128)(2,1)} %slice.151), channel_id=1, source_target_pairs={{0,1},{1,0},{2,3},{3,2},{4,5},{5,4},{6,7},{7,6},{8,9},{9,8},{10,11... | collective-permute-start | bytes 3538952 | tf_op jit(solution)/shard_map/ppermute | solution.py:385
  138.3 41.9 %collective-permute-start.4 = (bf16[8,64,1152]{2,1,0:T(8,128)(2,1)S(1)}, bf16[8,64,1152]{2,1,0:T(8,128)(2,1)S(1)}, u32[]{:S(2)}, u32[]{:S(2)}) collective-permute-start(bf16[8,64,1152]{2,1,0:T(8,128)(2,1)S(1)} %slice.107), channel_id=1, source_target_pairs={{0,1},{1,0},{2,3},{3,2},{4,5},{5,4},{6,7},{7,6},{8,9},{9,8},{10,11... | collective-permute-start | bytes 3538952 | tf_op jit(solution)/shard_map/ppermute | solution.py:385
  139.4 38.9 %collective-permute-start.15 = (bf16[4,96,768]{2,1,0:T(8,128)(2,1)S(1)}, bf16[4,96,768]{2,1,0:T(8,128)(2,1)S(1)}, u32[]{:S(2)}, u32[]{:S(2)}) collective-permute-start(bf16[4,96,768]{2,1,0:T(8,128)(2,1)S(1)} %slice.145), channel_id=1, source_target_pairs={{0,1},{1,0},{2,3},{3,2},{4,5},{5,4},{6,7},{7,6},{8,9},{9,8},{10,11... | collective-permute-start | bytes 1769480 | tf_op jit(solution)/shard_map/ppermute | solution.py:385
  142.4 38.9 %collective-permute-start.25 = (bf16[4,96,768]{2,1,0:T(8,128)(2,1)S(1)}, bf16[4,96,768]{2,1,0:T(8,128)(2,1)S(1)}, u32[]{:S(2)}, u32[]{:S(2)}) collective-permute-start(bf16[4,96,768]{2,1,0:T(8,128)(2,1)S(1)} %slice.153), channel_id=1, source_target_pairs={{0,4},{1,5},{2,6},{3,7},{4,0},{5,1},{6,2},{7,3},{8,12},{9,13},{10,... | collective-permute-start | bytes 1769480 | tf_op jit(solution)/shard_map/ppermute | solution.py:385
  180.5 13.6 %collective-permute-start.5 = (bf16[4,64,1152]{2,1,0:T(8,128)(2,1)S(1)}, bf16[4,64,1152]{2,1,0:T(8,128)(2,1)S(1)}, u32[]{:S(2)}, u32[]{:S(2)}) collective-permute-start(bf16[4,64,1152]{2,1,0:T(8,128)(2,1)S(1)} %slice.137), channel_id=1, source_target_pairs={{0,4},{1,5},{2,6},{3,7},{4,0},{5,1},{6,2},{7,3},{8,12},{9,13},{10,... | collective-permute-start | bytes 1769480 | tf_op jit(solution)/shard_map/ppermute | solution.py:385
  181.2 62.6 %collective-permute-start.2 = (bf16[512,1536]{1,0:T(8,128)(2,1)S(1)}, bf16[512,1536]{1,0:T(8,128)(2,1)S(1)}, u32[]{:S(2)}, u32[]{:S(2)}) collective-permute-start(bf16[512,1536]{1,0:T(8,128)(2,1)S(1)} %slice_bitcast_fusion.2), channel_id=1, source_target_pairs={{0,2},{1,3},{2,0},{3,1},{4,6},{5,7},{6,4},{7,5},{8,10},{9,11},{10,... | collective-permute-start | bytes 4718600 | tf_op jit(solution)/shard_map/ppermute | solution.py:385
  181.4 13.8 %collective-permute-start.26 = (bf16[2,96,768]{2,1,0:T(8,128)(2,1)S(1)}, bf16[2,96,768]{2,1,0:T(8,128)(2,1)S(1)}, u32[]{:S(2)}, u32[]{:S(2)}) collective-permute-start(bf16[2,96,768]{2,1,0:T(8,128)(2,1)S(1)} %slice.155), channel_id=1, source_target_pairs={{0,8},{1,9},{2,10},{3,11},{4,12},{5,13},{6,14},{7,15},{8,0},{9,1},... | collective-permute-start | bytes 884744 | tf_op jit(solution)/shard_map/ppermute | solution.py:385
  194.3 13.8 %collective-permute-start.6 = (bf16[2,64,1152]{2,1,0:T(8,128)(2,1)S(1)}, bf16[2,64,1152]{2,1,0:T(8,128)(2,1)S(1)}, u32[]{:S(2)}, u32[]{:S(2)}) collective-permute-start(bf16[2,64,1152]{2,1,0:T(8,128)(2,1)S(1)} %slice.139), channel_id=1, source_target_pairs={{0,8},{1,9},{2,10},{3,11},{4,12},{5,13},{6,14},{7,15},{8,0},{9,1},... | collective-permute-start | bytes 884744 | tf_op jit(solution)/shard_map/ppermute | solution.py:385
  198.3 17.1 %collective-permute-start.18 = (bf16[1,96,768]{2,1,0:T(8,128)(2,1)S(1)}, bf16[1,96,768]{2,1,0:T(8,128)(2,1)S(1)}, u32[]{:S(2)}, u32[]{:S(2)}) collective-permute-start(bf16[1,96,768]{2,1,0:T(8,128)(2,1)S(1)} %get-tuple-element.47), channel_id=1, source_target_pairs={{0,16},{1,17},{2,18},{3,19},{4,20},{5,21},{6,22},{7,23},{8,24},{9,... | collective-permute-start | bytes 442376 | tf_op jit(solution)/shard_map/ppermute | solution.py:385
  209.0 16.0 %collective-permute-start.28 = (bf16[1,96,768]{2,1,0:T(8,128)(2,1)S(1)}, bf16[1,96,768]{2,1,0:T(8,128)(2,1)S(1)}, u32[]{:S(2)}, u32[]{:S(2)}) collective-permute-start(bf16[1,96,768]{2,1,0:T(8,128)(2,1)S(1)} %get-tuple-element.45), channel_id=1, source_target_pairs={{0,16},{1,17},{2,18},{3,19},{4,20},{5,21},{6,22},{7,23},{8,24},{9,... | collective-permute-start | bytes 442376 | tf_op jit(solution)/shard_map/ppermute | solution.py:385
  215.4 17.6 %collective-permute-start.19 = (bf16[2,96,768]{2,1,0:T(8,128)(2,1)S(1)}, bf16[2,96,768]{2,1,0:T(8,128)(2,1)S(1)}, u32[]{:S(2)}, u32[]{:S(2)}) collective-permute-start(bf16[2,96,768]{2,1,0:T(8,128)(2,1)S(1)} %pad_maximum_fusion.7), channel_id=1, source_target_pairs={{0,8},{1,9},{2,10},{3,11},{4,12},{5,13},{6,14},{7,15},{8,0},{9,1},... | collective-permute-start | bytes 884744 | tf_op jit(solution)/shard_map/ppermute | solution.py:385
  233.1 27.0 %collective-permute-start.20 = (bf16[4,96,768]{2,1,0:T(8,128)(2,1)S(1)}, bf16[4,96,768]{2,1,0:T(8,128)(2,1)S(1)}, u32[]{:S(2)}, u32[]{:S(2)}) collective-permute-start(bf16[4,96,768]{2,1,0:T(8,128)(2,1)S(1)} %pad_maximum_fusion.4), channel_id=1, source_target_pairs={{0,1},{1,0},{2,3},{3,2},{4,5},{5,4},{6,7},{7,6},{8,9},{9,8},{10,11... | collective-permute-start | bytes 1769480 | tf_op jit(solution)/shard_map/ppermute | solution.py:385
  236.5 23.7 %collective-permute-start.30 = (bf16[4,96,768]{2,1,0:T(8,128)(2,1)S(1)}, bf16[4,96,768]{2,1,0:T(8,128)(2,1)S(1)}, u32[]{:S(2)}, u32[]{:S(2)}) collective-permute-start(bf16[4,96,768]{2,1,0:T(8,128)(2,1)S(1)} %pad_maximum_fusion.5), channel_id=1, source_target_pairs={{0,4},{1,5},{2,6},{3,7},{4,0},{5,1},{6,2},{7,3},{8,12},{9,13},{10,... | collective-permute-start | bytes 1769480 | tf_op jit(solution)/shard_map/ppermute | solution.py:385
  241.7 24.0 %collective-permute-start.10 = (bf16[4,64,1152]{2,1,0:T(8,128)(2,1)S(1)}, bf16[4,64,1152]{2,1,0:T(8,128)(2,1)S(1)}, u32[]{:S(2)}, u32[]{:S(2)}) collective-permute-start(bf16[4,64,1152]{2,1,0:T(8,128)(2,1)S(1)} %pad_maximum_fusion.3), channel_id=1, source_target_pairs={{0,4},{1,5},{2,6},{3,7},{4,0},{5,1},{6,2},{7,3},{8,12},{9,13},{10,... | collective-permute-start | bytes 1769480 | tf_op jit(solution)/shard_map/ppermute | solution.py:385
  245.3 71.7 %collective-permute-start.3 = (bf16[512,1536]{1,0:T(8,128)(2,1)}, bf16[512,1536]{1,0:T(8,128)(2,1)}, u32[]{:S(2)}, u32[]{:S(2)}) collective-permute-start(bf16[512,1536]{1,0:T(8,128)(2,1)} %fusion.2), channel_id=1, source_target_pairs={{0,0},{1,2},{2,1},{3,3},{4,4},{5,6},{6,5},{7,7},{8,8},{9,10},{10,9... | collective-permute-start | bytes 4718600 | tf_op jit(solution)/shard_map/ppermute | solution.py:536
  260.2 27.4 %collective-permute-start.21 = (bf16[8,96,768]{2,1,0:T(8,128)(2,1)S(1)}, bf16[8,96,768]{2,1,0:T(8,128)(2,1)S(1)}, u32[]{:S(2)}, u32[]{:S(2)}) collective-permute-start(bf16[8,96,768]{2,1,0:T(8,128)(2,1)S(1)} %pad_maximum_fusion.1), channel_id=1, source_target_pairs={{0,4},{1,5},{2,6},{3,7},{4,0},{5,1},{6,2},{7,3},{8,12},{9,13},{10,... | collective-permute-start | bytes 3538952 | tf_op jit(solution)/shard_map/ppermute | solution.py:385
  260.4 35.6 %collective-permute-start.31 = (bf16[8,96,768]{2,1,0:T(8,128)(2,1)S(1)}, bf16[8,96,768]{2,1,0:T(8,128)(2,1)S(1)}, u32[]{:S(2)}, u32[]{:S(2)}) collective-permute-start(bf16[8,96,768]{2,1,0:T(8,128)(2,1)S(1)} %pad_maximum_fusion.2), channel_id=1, source_target_pairs={{0,1},{1,0},{2,3},{3,2},{4,5},{5,4},{6,7},{7,6},{8,9},{9,8},{10,11... | collective-permute-start | bytes 3538952 | tf_op jit(solution)/shard_map/ppermute | solution.py:385
  265.9 50.7 %collective-permute-start.11 = (bf16[8,64,1152]{2,1,0:T(8,128)(2,1)S(1)}, bf16[8,64,1152]{2,1,0:T(8,128)(2,1)S(1)}, u32[]{:S(2)}, u32[]{:S(2)}) collective-permute-start(bf16[8,64,1152]{2,1,0:T(8,128)(2,1)S(1)} %pad_maximum_fusion), channel_id=1, source_target_pairs={{0,1},{1,0},{2,3},{3,2},{4,5},{5,4},{6,7},{7,6},{8,9},{9,8},{10,11... | collective-permute-start | bytes 3538952 | tf_op jit(solution)/shard_map/ppermute | solution.py:385
  288.6 63.4 %collective-permute-start.22 = (bf16[16,96,768]{2,1,0:T(8,128)(2,1)}, bf16[16,96,768]{2,1,0:T(8,128)(2,1)}, u32[]{:S(2)}, u32[]{:S(2)}) collective-permute-start(bf16[16,96,768]{2,1,0:T(8,128)(2,1)} %constant_dynamic-update-slice_fusion.5.own_ref), channel_id=1, source_target_pairs={{0,2},{1,3},{2,0},{3,1},{4,6},{5,7},{6,4},{7,5},{8,10},{9,11},{10,... | collective-permute-start | bytes 7077896 | tf_op jit(solution)/shard_map/ppermute | solution.py:385
  297.1 47.2 %collective-permute-start.32 = (bf16[16,96,768]{2,1,0:T(8,128)(2,1)}, bf16[16,96,768]{2,1,0:T(8,128)(2,1)}, u32[]{:S(2)}, u32[]{:S(2)}) collective-permute-start(bf16[16,96,768]{2,1,0:T(8,128)(2,1)} %constant_dynamic-update-slice_fusion.10.own_ref), channel_id=1, source_target_pairs={{0,2},{1,3},{2,0},{3,1},{4,6},{5,7},{6,4},{7,5},{8,10},{9,11},{10,... | collective-permute-start | bytes 7077896 | tf_op jit(solution)/shard_map/ppermute | solution.py:385
  316.8 43.1 %collective-permute-start.12 = (bf16[16,64,1152]{2,1,0:T(8,128)(2,1)S(1)}, bf16[16,64,1152]{2,1,0:T(8,128)(2,1)}, u32[]{:S(2)}, u32[]{:S(2)}) collective-permute-start(bf16[16,64,1152]{2,1,0:T(8,128)(2,1)S(1)} %constant_dynamic-update-slice_fusion.own_ref), channel_id=1, source_target_pairs={{0,2},{1,3},{2,0},{3,1},{4,6},{5,7},{6,4},{7,5},{8,10},{9,11},{10,... | collective-permute-start | bytes 7077896 | tf_op jit(solution)/shard_map/ppermute | solution.py:385
  (22 other events, 244.6 us)
